TPU v7x, 32 devices: a whole 2x2x4 slice. The times are simulated.
32 devices in a mesh: mp: 8 (over y, x, core), hidden: 4 (over z).
Axes of the slice: x: 2, y: 2, z: 4, core: 2. Of those that a mesh axis runs over, the one named last changes fastest.
Arguments:
- states: bfloat16 [512, 16384], P(None, 'mp'), may hold values from -6 to 6
- gate_codes: bfloat16 [16384, 26624], P('mp', 'hidden'), may hold values from -127 to 127, as said below
- gate_scales: float32 [128, 26624], P('mp', 'hidden'), may hold values from 7.8125e-05 to 0.000703125
- up_codes: bfloat16 [16384, 26624], P('mp', 'hidden'), may hold values from -127 to 127, as said below
- up_scales: float32 [128, 26624], P('mp', 'hidden'), may hold values from 7.8125e-05 to 0.000703125
- down_codes: bfloat16 [26624, 16384], P('hidden', 'mp'), may hold values from -127 to 127, as said below
- down_scales: float32 [208, 16384], P('hidden', 'mp'), may hold values from 1.2257258e-05 to 0.000110315326
Outputs:
- output: bfloat16 [512, 16384], P(None, 'mp')
Inputs may be any that keep to these rules, and one draw needn't show every extreme that they name: `gate_codes`: whole numbers. `up_codes`: whole numbers. `down_codes`: whole numbers.
All inputs are finite; a program needn't handle non-finite values. Where the computation divides by a largest or mean magnitude, that divisor is 1e-20 or more.
Results may differ from a plain program's by a relative error of at most 0.02.
Values may be sent and summed in bfloat16 or wider, within the bound.
A program may use at most 256 MiB of HBM per device.

v0:
```python
import functools

import jax
import jax.numpy as jnp
from jax import lax
from jax.experimental import pallas as pl
from jax.experimental.pallas import tpu as pltpu
from jax.sharding import PartitionSpec as P

F32, BF16 = jnp.float32, jnp.bfloat16
MESH = pl.DeviceIdType.MESH
SPLITS = 2
SLOTS = 4


def dequant(codes, scales):
    depth, columns = codes.shape
    groups = scales.shape[0]
    blocks = codes.astype(F32).reshape(groups, depth // groups, columns)
    return (blocks * scales.reshape(groups, 1, columns)).reshape(depth, columns).astype(BF16)


class Plan:
    def __init__(self, n, nz, rows, depth, hidden):
        self.n, self.nz, self.depth, self.hidden = n, nz, depth, hidden
        self.nb = n.bit_length() - 1
        self.h = SPLITS
        self.rb = rows // n // SPLITS
        self.w = next(t for t in (512, 256) if hidden % t == 0)
        self.wq = self.w // 2
        self.c = hidden // self.w
        self.u = self.c * self.h
        self.j = depth // self.wq
        self.v = self.j * self.h
        self.k2 = hidden // 2
        self.wrows = max(2 * depth, self.k2)
        dims = list(range(self.nb))
        self.orders = (dims, dims[:1] + dims[:0:-1])
        self.mid = nz // 2

    def left(self, q, k):
        return sorted(set(range(self.nb)) - set(self.orders[q][: k + 1]))

    def mask(self, pos):
        return sum(((pos >> (self.nb - 1 - d)) & 1) << d for d in range(self.nb))


def kernel(p, x_hbm, gc, uc, dc, gs, us, ds, out, xp, w, ps, r0, rk, act, zs, zr, zx, zf, sems):
    n, nb, C, U, J, V, rb, wq = p.n, p.nb, p.c, p.u, p.j, p.v, p.rb, p.wq
    me = lax.axis_index("mp").astype(jnp.int32)
    z = lax.axis_index("hidden").astype(jnp.int32)
    nz = p.nz
    on_left = z < p.mid
    deep = jnp.where(on_left, z, nz - 1 - z)
    inward = jnp.where(on_left, z + 1, z - 1)
    outward = jnp.where(on_left, z - 1, z + 1)
    every = slice(None)

    def index(fixed, dims):
        return tuple(fixed.get(d, every) for d in dims)

    def x_copy(h, pos):
        return pltpu.make_async_copy(x_hbm.at[me ^ p.mask(pos), h], xp.at[h, pos], sems["x"].at[h * n + pos])

    def w_copy(c, i):
        slot = lax.rem(c, 2)
        columns = pl.ds(pl.multiple_of(c * p.w, p.w), p.w)
        return pltpu.make_async_copy(
            (gc, uc)[i].at[:, columns], w.at[slot, pl.ds(i * p.depth, p.depth)], sems["w"].at[slot, i]
        )

    def d_copy(v, i):
        slot = lax.rem(v, 2)
        columns = pl.ds(pl.multiple_of(lax.rem(v, J) * wq, wq), wq)
        return pltpu.make_async_copy(
            dc.at[pl.ds(i * p.k2, p.k2), columns],
            w.at[slot, pl.ds(0, p.k2), pl.ds(i * wq, wq)],
            sems["w"].at[slot, i],
        )

    def remote(src, dst, send, recv, to):
        return pltpu.make_async_remote_copy(
            src_ref=src, dst_ref=dst, send_sem=send, recv_sem=recv, device_id=to, device_id_type=MESH
        )

    def part_at(u, q, fixed):
        return (u,) + index(fixed, range(nb)) + (q,)

    def sum_copy(s, q):
        d = p.orders[q][s]

        def make(u):
            slot = lax.rem(u, SLOTS)
            to = (me ^ (1 << d), z)
            if s == 0:
                return remote(ps.at[u, 1], r0.at[u], sems["s0"].at[slot], sems["r0"].at[u], to)
            fixed = {e: 0 for e in p.orders[q][:s]} | {d: 1}
            return remote(
                ps.at[part_at(u, q, fixed)],
                rk[s - 1].at[u, q],
                sems["sk"].at[s - 1, q, slot],
                sems["rk"].at[s - 1, q, u],
                to,
            )

        return make

    def act_copy(k, q):
        d = p.orders[q][nb - 1 - k]
        whole = p.orders[q][nb - k :]

        def make(u):
            slot = lax.rem(u, SLOTS)
            h, c = u // C, lax.rem(u, C)
            to = (me ^ (1 << d), z)
            last = k == nb - 1
            size = p.w if last else wq
            first = c * p.w + (0 if last else q * wq)
            columns = pl.ds(pl.multiple_of(first, wq), size)
            spots = [tuple(every if e in whole else (b if e == d else 0) for e in range(nb)) for b in (0, 1)]
            src, dst = (act.at[(h,) + spot + (every, columns)] for spot in spots)
            if last:
                return remote(src, dst, sems["sl"].at[slot], sems["rl"].at[u], to)
            return remote(src, dst, sems["sa"].at[k, q, slot], sems["ra"].at[k, q, u], to)

        return make

    def issue(make, u):
        @pl.when(u >= SLOTS)
        def _():
            make(u - SLOTS).wait_send()

        make(u).start()

    for i in range(2):
        w_copy(0, i).start()
    for h in range(p.h):
        for pos in range(n):
            x_copy(h, pos).start()
    barrier = pltpu.get_barrier_semaphore()
    for d in range(nb):
        pl.semaphore_signal(barrier, inc=1, device_id=(me ^ (1 << d), z), device_id_type=MESH)
    pl.semaphore_signal(barrier, inc=1, device_id=(me, inward), device_id_type=MESH)

    @pl.when(deep > 0)
    def _():
        pl.semaphore_signal(barrier, inc=1, device_id=(me, outward), device_id_type=MESH)

    pl.semaphore_wait(barrier, nb + 1 + jnp.where(deep > 0, 1, 0))
    for h in range(p.h):
        for pos in range(n):
            x_copy(h, pos).wait()

    def up(c):
        @pl.when(c + 1 < C)
        def _():
            for i in range(2):
                w_copy(c + 1, i).start()

        slot = lax.rem(c, 2)
        columns = pl.ds(pl.multiple_of(c * p.w, p.w), p.w)
        x = xp[...].reshape(p.h * n * rb, p.depth)
        for i, scales in enumerate((gs, us)):
            w_copy(c, i).wait()
            weight = dequant(w[slot, i * p.depth : (i + 1) * p.depth], scales[:, columns])
            part = jnp.dot(x, weight, preferred_element_type=F32).astype(BF16)
            part = part.reshape((p.h,) + (2,) * nb + (rb, p.w))
            for h in range(p.h):
                for q in range(2):
                    ps[(h * C + c,) + (every,) * nb + (q, i)] = part[h, ..., q * wq : (q + 1) * wq]

    def total(u, q, fixed, count):
        value = ps[part_at(u, q, fixed)].astype(F32)
        if count > 0:
            value = value + r0[(u,) + index(fixed, range(1, nb)) + (q,)].astype(F32)
        for k in range(1, count):
            value = value + rk[k - 1][(u, q) + index(fixed, p.left(q, k))].astype(F32)
        return value

    def reduce(s, u):
        if s == 1:
            sum_copy(0, 0)(u).wait_recv()
        for q in range(2):
            if s > 1:
                sum_copy(s - 1, q)(u).wait_recv()
            fixed = {e: 0 for e in p.orders[q][:s]} | {p.orders[q][s]: 1}
            ps[part_at(u, q, fixed)] = total(u, q, fixed, s).astype(BF16)
            issue(sum_copy(s, q), u)

    def activate(u):
        h, c = u // C, lax.rem(u, C)
        for q in range(2):
            sum_copy(nb - 1, q)(u).wait_recv()
            both = total(u, q, {e: 0 for e in range(nb)}, nb)
            gate, up_ = both[0], both[1]
            columns = pl.ds(pl.multiple_of(c * p.w + q * wq, wq), wq)
            act[(h,) + (0,) * nb + (every, columns)] = (gate / (1.0 + jnp.exp(-gate)) * up_).astype(BF16)
            issue(act_copy(0, q), u)

    def gather(k, u):
        for q in range(2):
            act_copy(k - 1, q)(u).wait_recv()
            if k < nb - 1:
                issue(act_copy(k, q), u)
        if k == nb - 1:
            issue(act_copy(k, 0), u)

    def down(v):
        @pl.when(v + 1 < V)
        def _():
            for i in range(2):
                d_copy(v + 1, i).start()

        h = v // J
        slot = lax.rem(v, 2)
        columns = pl.ds(pl.multiple_of(lax.rem(v, J) * wq, wq), wq)
        groups = ds.shape[0] // 2
        value = None
        for i in range(2):
            d_copy(v, i).wait()
            weight = dequant(
                w[slot, : p.k2, i * wq : (i + 1) * wq], ds[i * groups : (i + 1) * groups, columns]
            )
            a = act[(h,) + (every,) * nb + (every, slice(i * p.k2, (i + 1) * p.k2))].reshape(n * rb, p.k2)
            term = jnp.dot(a, weight, preferred_element_type=F32)
            value = term if value is None else value + term
        zs[v] = value.astype(BF16)

        @pl.when(deep == 0)
        def _():
            z_in(v).start()

    def z_in(v):
        return remote(zs.at[v], zr.at[v], sems["zs"].at[v], sems["zr"].at[v], (me, inward))

    def z_cross(v):
        return remote(zs.at[v], zx.at[v], sems["zs"].at[v], sems["zx"].at[v], (me, inward))

    def z_out(v):
        return remote(zf.at[v], zf.at[v], sems["zo"].at[v], sems["zf"].at[v], (me, outward))

    def put(v):
        h = v // J
        columns = pl.ds(pl.multiple_of(lax.rem(v, J) * wq, wq), wq)
        for pos in range(n):
            out[me ^ p.mask(pos), h, :, columns] = zf[v, pos * rb : (pos + 1) * rb]

    def z_step(k, v):
        if k < p.mid:

            @pl.when(deep == k)
            def _():
                z_in(v).wait_recv()
                zs[v] = (zs[v].astype(F32) + zr[v].astype(F32)).astype(BF16)
                if k < p.mid - 1:
                    z_in(v).start()
                else:
                    z_cross(v).start()
        elif k == p.mid:

            @pl.when(deep == p.mid - 1)
            def _():
                z_cross(v).wait_recv()
                h = v // J
                columns = pl.ds(pl.multiple_of(lax.rem(v, J) * wq, wq), wq)
                own = xp[h, :, :, columns].reshape(n * rb, wq).astype(F32)
                zf[v] = (zs[v].astype(F32) + zx[v].astype(F32) + own).astype(BF16)
                if p.mid > 1:
                    z_out(v).start()
                put(v)
        else:
            at = 2 * p.mid - 1 - k

            @pl.when(deep == at)
            def _():
                z_out(v).wait_recv()
                if at > 0:
                    z_out(v).start()
                put(v)

    first_down = C + 2 * nb

    def item(t, run):
        h, j = jnp.maximum(t, 0) // C, lax.rem(jnp.maximum(t, 0), C)

        @pl.when((t >= 0) & (h < p.h) & (j < J))
        def _():
            run(h * J + j)

    def unit(u, run):
        @pl.when((u >= 0) & (u < U))
        def _():
            run(u)

    def step(t, carry):
        @pl.when(t < C)
        def _():
            up(t)

        @pl.when(t == C)
        def _():
            for i in range(2):
                d_copy(0, i).start()

        item(t - first_down, down)
        unit(t, lambda u: issue(sum_copy(0, 0), u))
        for s in range(1, nb):
            unit(t - s, functools.partial(reduce, s))
        unit(t - nb, activate)
        for k in range(1, nb):
            unit(t - nb - k, functools.partial(gather, k))
        unit(t - 2 * nb, lambda u: act_copy(nb - 1, 0)(u).wait_recv())
        for k in range(1, 2 * p.mid):
            item(t - first_down - k, functools.partial(z_step, k))
        return carry

    lax.fori_loop(0, first_down + (p.h - 1) * C + J + 2 * p.mid - 1, step, 0)

    for u in range(U - SLOTS, U):
        sum_copy(0, 0)(u).wait_send()
        act_copy(nb - 1, 0)(u).wait_send()
        for q in range(2):
            for s in range(1, nb):
                sum_copy(s, q)(u).wait_send()
            for k in range(nb - 1):
                act_copy(k, q)(u).wait_send()

    def finish(v, carry):
        z_in(v).wait_send()

        @pl.when(deep > 0)
        def _():
            z_out(v).wait_send()

        return carry

    lax.fori_loop(0, V, finish, 0)


def body(n, nz, states, gc, gs, uc, us, dc, ds):
    rows, depth = states.shape
    hidden = gc.shape[1]
    p = Plan(n, nz, rows, depth, hidden)
    nb, U, V, rb, wq = p.nb, p.u, p.v, p.rb, p.wq
    dma = pltpu.SemaphoreType.DMA
    vmem = pl.BlockSpec(memory_space=pltpu.VMEM)
    hbm = pl.BlockSpec(memory_space=pl.ANY)
    two = (2,) * nb
    item = (V, n * rb, wq)
    scratch = [
        pltpu.VMEM((p.h, n, rb, depth), BF16),
        pltpu.VMEM((2, p.wrows, p.w), BF16),
        pltpu.VMEM((U,) + two + (2, 2, rb, wq), BF16),
        pltpu.VMEM((U,) + two[1:] + (2, 2, rb, wq), BF16),
        [pltpu.VMEM((U, 2) + two[k + 1 :] + (2, rb, wq), BF16) for k in range(1, nb)],
        pltpu.VMEM((p.h,) + two + (rb, hidden), BF16),
        pltpu.VMEM(item, BF16),
        pltpu.VMEM(item, BF16),
        pltpu.VMEM(item, BF16),
        pltpu.VMEM(item, BF16),
        {
            "x": dma((p.h * n,)),
            "w": dma((2, 2)),
            "s0": dma((SLOTS,)),
            "r0": dma((U,)),
            "sk": dma((nb - 1, 2, SLOTS)),
            "rk": dma((nb - 1, 2, U)),
            "sa": dma((nb - 1, 2, SLOTS)),
            "ra": dma((nb - 1, 2, U)),
            "sl": dma((SLOTS,)),
            "rl": dma((U,)),
            "zs": dma((V,)),
            "zr": dma((V,)),
            "zx": dma((V,)),
            "zo": dma((V,)),
            "zf": dma((V,)),
        },
    ]
    out = pl.pallas_call(
        functools.partial(kernel, p),
        out_shape=jax.ShapeDtypeStruct((n, p.h, rb, depth), BF16),
        in_specs=[hbm] * 4 + [vmem] * 3,
        out_specs=vmem,
        scratch_shapes=scratch,
        compiler_params=pltpu.CompilerParams(collective_id=0, has_side_effects=True, vmem_limit_bytes=67043328),
        cost_estimate=pl.CostEstimate(
            flops=6 * rows * depth * hidden, bytes_accessed=8 * depth * hidden, transcendentals=0
        ),
        name="mlp",
    )(states.reshape(n, p.h, rb, depth), gc, uc, dc, gs, us, ds)
    return out.reshape(rows, depth)


def solution(mesh):
    in_specs = (
        P(None, "mp"),
        P("mp", "hidden"),
        P("mp", "hidden"),
        P("mp", "hidden"),
        P("mp", "hidden"),
        P("hidden", "mp"),
        P("hidden", "mp"),
    )
    return jax.shard_map(
        functools.partial(body, mesh.shape["mp"], mesh.shape["hidden"]),
        mesh=mesh,
        in_specs=in_specs,
        out_specs=P(None, "mp"),
        check_vma=False,
    )
```

profile of v0, /device:TPU:0, one launch (start us, length us, event | category | flops | bytes accessed | tf_op | source)
XLA Modules:
  0.0 165.1 jit_solution(7158643757660960888)
XLA Ops:
  0.0 161.9 %mlp.1 = bf16[8,2,32,2048]{3,2,1,0:T(8,128)(2,1)} custom-call(bf16[8,2,32,2048]{3,2,1,0:T(8,128)(2,1)} %bitcast.3, bf16[2048,6656]{1,0:T(8,128)(2,1)} %gc.1, bf16[2048,6656]{1,0:T(8,128)(2,1)} %uc.1, bf16[6656,2048]{1,0:T(8,128)(2,1)} %dc.1, f32[16,6656]{1,0:T(8,128)} %gs.1, f32[16,6656]{1,0:T(8,128)} %us.1, f32[52,2048]{1,0:T(8,128)} %ds.1), custom_call_target="tpu_custom_call" | custom-call | flops 41875931136 | bytes 109051904 | tf_op jit(solution)/shard_map/mlp/pallas_call | solution.py:379
  161.9 3.2 %copy.9 = bf16[512,2048]{1,0:T(8,128)(2,1)} copy(bf16[512,2048]{1,0:T(8,128)(2,1)} %bitcast.2) | data formatting | bytes 4194304
where the time goes:
time: 165 us
  Pallas kernels  162 us (98%)
  local copies, waits for them, and re-layouts  3.16 us (2%)
    pallas_call x1, Pallas kernels, body(): pl.pallas_call(functools.partial(kernel, p), out_shape=jax.ShapeDtypeStru...  162 us

commit v1 on v0

v1 whole, which is shorter than its diff:
```python
import functools

import jax
import jax.numpy as jnp
from jax import lax
from jax.experimental import pallas as pl
from jax.experimental.pallas import tpu as pltpu
from jax.sharding import PartitionSpec as P

F32, BF16 = jnp.float32, jnp.bfloat16
MESH = pl.DeviceIdType.MESH
SLOTS = 4
SPLITS = ((2, 1, 1), (1, 1))
PACES = (1, 2, 2)
EARLY = (0, 0, 0)
FIRST = 0
LAGS = (4, 6, 6)


def dequant(codes, scales):
    depth, columns = codes.shape
    groups = scales.shape[0]
    blocks = codes.astype(F32).reshape(groups, depth // groups, columns)
    return (blocks * scales.reshape(groups, 1, columns)).reshape(depth, columns).astype(BF16)


class Split:
    def __init__(self, rb, row, off, runs, lag, pace):
        self.rb, self.row, self.off, self.runs, self.lag = rb, row, off, runs, lag
        self.send, self.recv = 2 * pace, 4 * pace


class Plan:
    def __init__(self, n, nz, rows, depth, hidden):
        self.n, self.nz, self.depth, self.hidden = n, nz, depth, hidden
        self.nb = n.bit_length() - 1
        self.rows = rows
        self.w = next(t for t in (512, 256) if hidden % t == 0)
        self.wq = self.w // 2
        self.c = hidden // self.w
        self.j = depth // self.wq
        self.k2 = hidden // 2
        self.wrows = max(2 * depth, self.k2)
        dims = list(range(self.nb))
        self.orders = (dims, dims[:1] + dims[:0:-1])
        self.mid = nz // 2
        rb = rows // n
        parts = next((p for p in SPLITS if all(rb * a % (16 * sum(p)) == 0 for a in p)), (1,))
        self.splits = []
        row, free, tick = 0, 0, 0
        for i, a in enumerate(parts):
            size = rb * a // sum(parts)
            pace = PACES[i] if i else 1
            early = min(EARLY[i], self.c) if i else 0
            runs = []
            if early:
                runs.append((0, early, FIRST, 1))
            if early < self.c:
                runs.append((early, self.c, tick, pace))
                tick += -(-(self.c - early) // pace)
            split = Split(size, row, n * row, runs, LAGS[i], pace)
            split.down = max(tick + 2 * self.nb, free)
            free = split.down + self.j
            self.splits.append(split)
            row += size
        self.cuts = {0, self.c} | {s.down for s in self.splits} | {s.down + self.j for s in self.splits}
        self.ticks = max(s.down + self.j - 1 + self.after(s, 2 * self.mid - 1) for s in self.splits) + 1

    def after(self, s, k):
        return -(-s.lag * k // 2)

    def left(self, q, k):
        return sorted(set(range(self.nb)) - set(self.orders[q][: k + 1]))

    def mask(self, pos):
        return sum(((pos >> (self.nb - 1 - d)) & 1) << d for d in range(self.nb))


def kernel(p, x_hbm, gc, uc, dc, gs, us, ds, out_hbm, out, xp, w, per, sems):
    n, nb, C, J, wq = p.n, p.nb, p.c, p.j, p.wq
    me = lax.axis_index("mp").astype(jnp.int32)
    z = lax.axis_index("hidden").astype(jnp.int32)
    nz = p.nz
    on_left = z < p.mid
    deep = jnp.where(on_left, z, nz - 1 - z)
    inward = jnp.where(on_left, z + 1, z - 1)
    outward = jnp.where(on_left, z - 1, z + 1)
    every = slice(None)

    def index(fixed, dims):
        return tuple(fixed.get(d, every) for d in dims)

    def columns_of(c):
        return pl.ds(pl.multiple_of(c * p.w, p.w), p.w)

    def columns_at(j):
        return pl.ds(pl.multiple_of(j * wq, wq), wq)

    def x_copy(i, pos):
        s = p.splits[i]
        return pltpu.make_async_copy(
            x_hbm.at[me ^ p.mask(pos), pl.ds(s.row, s.rb)],
            xp.at[pl.ds(s.off + pos * s.rb, s.rb)],
            sems["x"].at[i * n + pos],
        )

    def w_copy(c, i):
        slot = lax.rem(c, 2)
        return pltpu.make_async_copy(
            (gc, uc)[i].at[:, columns_of(c)], w.at[slot, pl.ds(i * p.depth, p.depth)], sems["w"].at[slot, i]
        )

    def d_copy(v, i):
        slot = lax.rem(v, 2)
        return pltpu.make_async_copy(
            dc.at[pl.ds(i * p.k2, p.k2), columns_at(lax.rem(v, J))],
            w.at[slot, pl.ds(0, p.k2), pl.ds(i * wq, wq)],
            sems["w"].at[slot, i],
        )

    def out_copy(i, j):
        s = p.splits[i]
        part = (every, pl.ds(s.row, s.rb), columns_at(j))
        return pltpu.make_async_copy(out.at[part], out_hbm.at[part], per[i]["sem"]["o"].at[lax.rem(j, SLOTS)])

    def remote(src, dst, send, recv, to):
        return pltpu.make_async_remote_copy(
            src_ref=src, dst_ref=dst, send_sem=send, recv_sem=recv, device_id=to, device_id_type=MESH
        )

    def part_at(c, q, fixed):
        return (c,) + index(fixed, range(nb)) + (q,)

    def sum_copy(i, s, q):
        d = p.orders[q][s]
        ps, r0, rk, sem = per[i]["ps"], per[i]["r0"], per[i]["rk"], per[i]["sem"]

        def make(c):
            slot, got = lax.rem(c, p.splits[i].send), lax.rem(c, p.splits[i].recv)
            to = (me ^ (1 << d), z)
            if s == 0:
                return remote(ps.at[c, 1], r0.at[c], sem["s0"].at[slot], sem["r0"].at[got], to)
            fixed = {e: 0 for e in p.orders[q][:s]} | {d: 1}
            return remote(
                ps.at[part_at(c, q, fixed)],
                rk[s - 1].at[c, q],
                sem["sk"].at[s - 1, q, slot],
                sem["rk"].at[s - 1, q, got],
                to,
            )

        return make

    def act_copy(i, k, q):
        d = p.orders[q][nb - 1 - k]
        whole = p.orders[q][nb - k :]
        act, sem = per[i]["act"], per[i]["sem"]

        def make(c):
            slot, got = lax.rem(c, p.splits[i].send), lax.rem(c, p.splits[i].recv)
            to = (me ^ (1 << d), z)
            last = k == nb - 1
            size = p.w if last else wq
            first = c * p.w + (0 if last else q * wq)
            columns = pl.ds(pl.multiple_of(first, wq), size)
            spots = [tuple(every if e in whole else (b if e == d else 0) for e in range(nb)) for b in (0, 1)]
            src, dst = (act.at[spot + (every, columns)] for spot in spots)
            if last:
                return remote(src, dst, sem["sl"].at[slot], sem["rl"].at[got], to)
            return remote(src, dst, sem["sa"].at[k, q, slot], sem["ra"].at[k, q, got], to)

        return make

    def issue(make, c, slots):
        @pl.when(c >= slots)
        def _():
            make(c - slots).wait_send()

        make(c).start()

    for i in range(len(p.splits)):
        for pos in range(n):
            x_copy(i, pos).start()
    for i in range(2):
        w_copy(0, i).start()
    barrier = pltpu.get_barrier_semaphore()
    for d in range(nb):
        pl.semaphore_signal(barrier, inc=1, device_id=(me ^ (1 << d), z), device_id_type=MESH)
    pl.semaphore_signal(barrier, inc=1, device_id=(me, inward), device_id_type=MESH)

    @pl.when(deep > 0)
    def _():
        pl.semaphore_signal(barrier, inc=1, device_id=(me, outward), device_id_type=MESH)

    for i in range(len(p.splits)):
        for pos in range(n):
            x_copy(i, pos).wait()
    pl.semaphore_wait(barrier, nb + 1 + jnp.where(deep > 0, 1, 0))

    def up(c):
        @pl.when(c + 1 < C)
        def _():
            for i in range(2):
                w_copy(c + 1, i).start()

        slot = lax.rem(c, 2)
        for i, scales in enumerate((gs, us)):
            w_copy(c, i).wait()
            weight = dequant(w[slot, i * p.depth : (i + 1) * p.depth], scales[:, columns_of(c)])
            part = jnp.dot(xp[...], weight, preferred_element_type=F32).astype(BF16)
            for s, own in zip(p.splits, per):
                rows = part[s.off : s.off + n * s.rb].reshape((2,) * nb + (s.rb, p.w))
                for q in range(2):
                    own["ps"][(c,) + (every,) * nb + (q, i)] = rows[..., q * wq : (q + 1) * wq]

    def total(own, c, q, fixed, count):
        value = own["ps"][part_at(c, q, fixed)].astype(F32)
        if count > 0:
            value = value + own["r0"][(c,) + index(fixed, range(1, nb)) + (q,)].astype(F32)
        for k in range(1, count):
            value = value + own["rk"][k - 1][(c, q) + index(fixed, p.left(q, k))].astype(F32)
        return value

    def reduce(i, s, c):
        if s == 1:
            sum_copy(i, 0, 0)(c).wait_recv()
        for q in range(2):
            if s > 1:
                sum_copy(i, s - 1, q)(c).wait_recv()
            fixed = {e: 0 for e in p.orders[q][:s]} | {p.orders[q][s]: 1}
            per[i]["ps"][part_at(c, q, fixed)] = total(per[i], c, q, fixed, s).astype(BF16)
            issue(sum_copy(i, s, q), c, p.splits[i].send)

    def activate(i, c):
        for q in range(2):
            sum_copy(i, nb - 1, q)(c).wait_recv()
            both = total(per[i], c, q, {e: 0 for e in range(nb)}, nb)
            gate, up_ = both[0], both[1]
            columns = pl.ds(pl.multiple_of(c * p.w + q * wq, wq), wq)
            per[i]["act"][(0,) * nb + (every, columns)] = (gate / (1.0 + jnp.exp(-gate)) * up_).astype(BF16)
            issue(act_copy(i, 0, q), c, p.splits[i].send)

    def gather(i, k, c):
        for q in range(2):
            act_copy(i, k - 1, q)(c).wait_recv()
            if k < nb - 1:
                issue(act_copy(i, k, q), c, p.splits[i].send)
        if k == nb - 1:
            issue(act_copy(i, k, 0), c, p.splits[i].send)

    def down(i, j):
        v = i * J + j

        @pl.when(v + 1 < J * len(p.splits))
        def _():
            for k in range(2):
                d_copy(v + 1, k).start()

        own = per[i]
        slot = lax.rem(v, 2)
        groups = ds.shape[0] // 2
        value = None
        for k in range(2):
            d_copy(v, k).wait()
            weight = dequant(
                w[slot, : p.k2, k * wq : (k + 1) * wq], ds[k * groups : (k + 1) * groups, columns_at(j)]
            )
            a = own["act"][(every,) * nb + (every, slice(k * p.k2, (k + 1) * p.k2))]
            term = jnp.dot(a.reshape(n * p.splits[i].rb, p.k2), weight, preferred_element_type=F32)
            value = term if value is None else value + term
        own["zs"][j] = value.astype(BF16)

        @pl.when(deep == 0)
        def _():
            issue(functools.partial(z_in, i), j, SLOTS)

    def z_in(i, j):
        own, sem = per[i], per[i]["sem"]
        return remote(own["zs"].at[j], own["zr"].at[j], sem["zs"].at[lax.rem(j, SLOTS)], sem["zr"].at[j], (me, inward))

    def z_cross(i, j):
        own, sem = per[i], per[i]["sem"]
        return remote(own["zs"].at[j], own["zx"].at[j], sem["zs"].at[lax.rem(j, SLOTS)], sem["zx"].at[j], (me, inward))

    def z_out(i, j):
        own, sem = per[i], per[i]["sem"]
        return remote(own["zf"].at[j], own["zf"].at[j], sem["zo"].at[lax.rem(j, SLOTS)], sem["zf" if p.mid > 2 else "zr"].at[j], (me, outward))

    def put(i, j):
        s = p.splits[i]
        for pos in range(n):
            out[me ^ p.mask(pos), s.row : s.row + s.rb, columns_at(j)] = per[i]["zf"][j, pos * s.rb : (pos + 1) * s.rb]

        @pl.when(j >= SLOTS)
        def _():
            out_copy(i, j - SLOTS).wait()

        out_copy(i, j).start()

    def z_step(i, k, j):
        zs, zr, zx, zf = (per[i][key] for key in ("zs", "zr", "zx", "zf"))
        if k < p.mid:

            @pl.when(deep == k)
            def _():
                z_in(i, j).wait_recv()
                zs[j] = (zs[j].astype(F32) + zr[j].astype(F32)).astype(BF16)
                if k < p.mid - 1:
                    issue(functools.partial(z_in, i), j, SLOTS)
                else:
                    issue(functools.partial(z_cross, i), j, SLOTS)
        elif k == p.mid:

            @pl.when(deep == p.mid - 1)
            def _():
                z_cross(i, j).wait_recv()
                s = p.splits[i]
                own = xp[s.off : s.off + n * s.rb, columns_at(j)].astype(F32)
                zf[j] = (zs[j].astype(F32) + zx[j].astype(F32) + own).astype(BF16)
                if p.mid > 1:
                    issue(functools.partial(z_out, i), j, SLOTS)
                put(i, j)
        else:
            at = 2 * p.mid - 1 - k

            @pl.when(deep == at)
            def _():
                z_out(i, j).wait_recv()
                if at > 0:
                    issue(functools.partial(z_out, i), j, SLOTS)
                put(i, j)

    def shift(s, k):
        return [(first, last, start + k, pace) for first, last, start, pace in s.runs]

    def each(t, begin, end, runs, run):
        for first, last, start, pace in runs:
            for g in range(pace):
                stop = start - (g - (last - first)) // pace
                if begin >= stop or end <= start:
                    continue
                i = first + (t - start) * pace + g
                if start <= begin and end <= stop:
                    run(i)
                else:
                    pl.when((t >= start) & (t < stop))(functools.partial(run, i))

    def step(begin, end, t, carry):
        act_ = functools.partial(each, t, begin, end)
        if end <= C:
            up(t)
        for i, s in enumerate(p.splits):
            act_([(0, J, s.down, 1)], functools.partial(down, i))
            act_(shift(s, 0), lambda c, i=i: issue(sum_copy(i, 0, 0), c, p.splits[i].send))
        for k in range(1, 2 * nb + 1):
            for i, s in enumerate(p.splits):
                if k < nb:
                    run = functools.partial(reduce, i, k)
                elif k == nb:
                    run = functools.partial(activate, i)
                elif k < 2 * nb:
                    run = functools.partial(gather, i, k - nb)
                else:
                    run = lambda c, i=i: act_copy(i, nb - 1, 0)(c).wait_recv()
                act_(shift(s, k), run)
        for k in range(1, 2 * p.mid):
            for i, s in enumerate(p.splits):
                act_([(0, J, s.down + p.after(s, k), 1)], functools.partial(z_step, i, k))
        return carry

    cuts = sorted(c for c in p.cuts if c < p.ticks) + [p.ticks]
    for begin, end in zip(cuts, cuts[1:]):
        if begin == C:
            for i in range(2):
                d_copy(0, i).start()
        lax.fori_loop(begin, end, functools.partial(step, begin, end), 0)

    for i in range(len(p.splits)):
        for c in range(max(C - p.splits[i].send, 0), C):
            sum_copy(i, 0, 0)(c).wait_send()
            act_copy(i, nb - 1, 0)(c).wait_send()
            for q in range(2):
                for s in range(1, nb):
                    sum_copy(i, s, q)(c).wait_send()
                for k in range(nb - 1):
                    act_copy(i, k, q)(c).wait_send()

        def finish(j, carry, i=i):
            z_in(i, j).wait_send()
            out_copy(i, j).wait()

            @pl.when(deep > 0)
            def _():
                z_out(i, j).wait_send()

            return carry

        lax.fori_loop(max(J - SLOTS, 0), J, finish, 0)


def body(n, nz, states, gc, gs, uc, us, dc, ds):
    rows, depth = states.shape
    hidden = gc.shape[1]
    p = Plan(n, nz, rows, depth, hidden)
    nb, C, J, wq = p.nb, p.c, p.j, p.wq
    dma = pltpu.SemaphoreType.DMA
    vmem = pl.BlockSpec(memory_space=pltpu.VMEM)
    hbm = pl.BlockSpec(memory_space=pl.ANY)
    two = (2,) * nb

    def own(s):
        item = pltpu.VMEM((J, n * s.rb, wq), BF16)
        return {
            "ps": pltpu.VMEM((C,) + two + (2, 2, s.rb, wq), BF16),
            "r0": pltpu.VMEM((C,) + two[1:] + (2, 2, s.rb, wq), BF16),
            "rk": [pltpu.VMEM((C, 2) + two[k + 1 :] + (2, s.rb, wq), BF16) for k in range(1, nb)],
            "act": pltpu.VMEM(two + (s.rb, hidden), BF16),
            "zs": item,
            "zr": item,
            "zx": item,
            "zf": item,
            "sem": {
                "s0": dma((s.send,)),
                "r0": dma((s.recv,)),
                "sk": dma((nb - 1, 2, s.send)),
                "rk": dma((nb - 1, 2, s.recv)),
                "sa": dma((nb - 1, 2, s.send)),
                "ra": dma((nb - 1, 2, s.recv)),
                "sl": dma((s.send,)),
                "rl": dma((s.recv,)),
                "zs": dma((SLOTS,)),
                "zr": dma((J,)),
                "zx": dma((J,)),
                "zo": dma((SLOTS,)),
                "zf": dma((J if p.mid > 2 else 1,)),
                "o": dma((SLOTS,)),
            },
        }

    out = pl.pallas_call(
        functools.partial(kernel, p),
        out_shape=jax.ShapeDtypeStruct((n, rows // n, depth), BF16),
        in_specs=[hbm] * 4 + [vmem] * 3,
        out_specs=hbm,
        scratch_shapes=[
            pltpu.VMEM((n, rows // n, depth), BF16),
            pltpu.VMEM((rows, depth), BF16),
            pltpu.VMEM((2, p.wrows, p.w), BF16),
            [own(s) for s in p.splits],
            {"x": dma((len(p.splits) * n,)), "w": dma((2, 2))},
        ],
        compiler_params=pltpu.CompilerParams(collective_id=0, has_side_effects=True, vmem_limit_bytes=67043328),
        cost_estimate=pl.CostEstimate(
            flops=6 * rows * depth * hidden, bytes_accessed=8 * depth * hidden, transcendentals=0
        ),
        name="mlp",
    )(states.reshape(n, rows // n, depth), gc, uc, dc, gs, us, ds)
    return out.reshape(rows, depth)


def solution(mesh):
    in_specs = (
        P(None, "mp"),
        P("mp", "hidden"),
        P("mp", "hidden"),
        P("mp", "hidden"),
        P("mp", "hidden"),
        P("hidden", "mp"),
        P("hidden", "mp"),
    )
    return jax.shard_map(
        functools.partial(body, mesh.shape["mp"], mesh.shape["hidden"]),
        mesh=mesh,
        in_specs=in_specs,
        out_specs=P(None, "mp"),
        check_vma=False,
    )
```

time: 165 us -> 146 us (0.88)
  Pallas kernels: 162 us -> 143 us
    pallas_call x1, Pallas kernels: 162 us -> 143 us  [body(): pl.pallas_call(functools.partial(kernel, p), out_shape=jax.ShapeDtypeStru...]
where the time goes in v1:
time: 146 us
  Pallas kernels  143 us (98%)
  local copies, waits for them, and re-layouts  3.16 us (2%)
    pallas_call x1, Pallas kernels, body(): pl.pallas_call(functools.partial(kernel, p), out_shape=jax.ShapeDtypeStru...  143 us
    unnamed x1, local copies, waits for them, and re-layouts  3.16 us

profile of v1, /device:TPU:0, one launch (start us, length us, event | category | flops | bytes accessed | tf_op | source)
XLA Modules:
  0.0 146.0 jit_solution(12477832023282671565)
XLA Ops:
  0.0 142.8 %mlp.1 = bf16[8,64,2048]{2,1,0:T(8,128)(2,1)} custom-call(bf16[8,64,2048]{2,1,0:T(8,128)(2,1)} %bitcast.3, bf16[2048,6656]{1,0:T(8,128)(2,1)} %gc.1, bf16[2048,6656]{1,0:T(8,128)(2,1)} %uc.1, bf16[6656,2048]{1,0:T(8,128)(2,1)} %dc.1, f32[16,6656]{1,0:T(8,128)} %gs.1, f32[16,6656]{1,0:T(8,128)} %us.1, f32[52,2048]{1,0:T(8,128)} %ds.1), custom_call_target="tpu_custom_call" | custom-call | flops 41875931136 | bytes 109051904 | tf_op jit(solution)/shard_map/mlp/pallas_call | solution.py:440
  142.8 3.2 %copy.9 = bf16[512,2048]{1,0:T(8,128)(2,1)} copy(bf16[512,2048]{1,0:T(8,128)(2,1)} %bitcast.2) | data formatting | bytes 4194304

commit v2 on v1

--- a/solution.py
+++ b/solution.py
@@ -12,9 +12,8 @@
 SLOTS = 4
 SPLITS = ((2, 1, 1), (1, 1))
 PACES = (1, 2, 2)
-EARLY = (0, 0, 0)
-FIRST = 0
-LAGS = (4, 6, 6)
+SLOW = (0, 3, 0)
+LAGS = (4, 6, 7)
 
 
 def dequant(codes, scales):
@@ -51,19 +50,20 @@
         for i, a in enumerate(parts):
             size = rb * a // sum(parts)
             pace = PACES[i] if i else 1
-            early = min(EARLY[i], self.c) if i else 0
+            slow = min(SLOW[i], self.c) if i else 0
             runs = []
-            if early:
-                runs.append((0, early, FIRST, 1))
-            if early < self.c:
-                runs.append((early, self.c, tick, pace))
-                tick += -(-(self.c - early) // pace)
+            if slow:
+                runs.append((0, slow, tick, 1))
+                tick += slow
+            if slow < self.c:
+                runs.append((slow, self.c, tick, pace))
+                tick += -(-(self.c - slow) // pace)
             split = Split(size, row, n * row, runs, LAGS[i], pace)
             split.down = max(tick + 2 * self.nb, free)
             free = split.down + self.j
             self.splits.append(split)
             row += size
-        self.cuts = {0, self.c} | {s.down for s in self.splits} | {s.down + self.j for s in self.splits}
+        self.cuts = {0, 1, self.c} | {s.down for s in self.splits} | {s.down + self.j for s in self.splits}
         self.ticks = max(s.down + self.j - 1 + self.after(s, 2 * self.mid - 1) for s in self.splits) + 1
 
     def after(self, s, k):
@@ -144,8 +144,8 @@
             return remote(
                 ps.at[part_at(c, q, fixed)],
                 rk[s - 1].at[c, q],
-                sem["sk"].at[s - 1, q, slot],
-                sem["rk"].at[s - 1, q, got],
+                sem["sk"].at[s - 1, slot],
+                sem["rk"].at[s - 1, got],
                 to,
             )
 
@@ -167,7 +167,7 @@
             src, dst = (act.at[spot + (every, columns)] for spot in spots)
             if last:
                 return remote(src, dst, sem["sl"].at[slot], sem["rl"].at[got], to)
-            return remote(src, dst, sem["sa"].at[k, q, slot], sem["ra"].at[k, q, got], to)
+            return remote(src, dst, sem["sa"].at[k, slot], sem["ra"].at[k, got], to)
 
         return make
 
@@ -177,6 +177,21 @@
             make(c - slots).wait_send()
 
         make(c).start()
+
+    def sums_wait(i, s, c, key, slots):
+        both = per[i]["rk"][s - 1].at[c]
+        pltpu.make_async_copy(both, both, per[i]["sem"][key].at[s - 1, lax.rem(c, slots)]).wait()
+
+    def acts_wait(i, k, c, key, slots):
+        both = per[i]["act"].at[(0,) * (nb - k) + (every,) * k + (every, columns_of(c))]
+        pltpu.make_async_copy(both, both, per[i]["sem"][key].at[k, lax.rem(c, slots)]).wait()
+
+    def make_room(wait, i, k, c, key):
+        slots = p.splits[i].send
+
+        @pl.when(c >= slots)
+        def _():
+            wait(i, k, c - slots, key, slots)
 
     for i in range(len(p.splits)):
         for pos in range(n):
@@ -195,7 +210,6 @@
     for i in range(len(p.splits)):
         for pos in range(n):
             x_copy(i, pos).wait()
-    pl.semaphore_wait(barrier, nb + 1 + jnp.where(deep > 0, 1, 0))
 
     def up(c):
         @pl.when(c + 1 < C)
@@ -224,28 +238,31 @@
     def reduce(i, s, c):
         if s == 1:
             sum_copy(i, 0, 0)(c).wait_recv()
+        else:
+            sums_wait(i, s - 1, c, "rk", p.splits[i].recv)
+        make_room(sums_wait, i, s, c, "sk")
         for q in range(2):
-            if s > 1:
-                sum_copy(i, s - 1, q)(c).wait_recv()
             fixed = {e: 0 for e in p.orders[q][:s]} | {p.orders[q][s]: 1}
             per[i]["ps"][part_at(c, q, fixed)] = total(per[i], c, q, fixed, s).astype(BF16)
-            issue(sum_copy(i, s, q), c, p.splits[i].send)
+            sum_copy(i, s, q)(c).start()
 
     def activate(i, c):
+        sums_wait(i, nb - 1, c, "rk", p.splits[i].recv)
+        make_room(acts_wait, i, 0, c, "sa")
         for q in range(2):
-            sum_copy(i, nb - 1, q)(c).wait_recv()
             both = total(per[i], c, q, {e: 0 for e in range(nb)}, nb)
             gate, up_ = both[0], both[1]
             columns = pl.ds(pl.multiple_of(c * p.w + q * wq, wq), wq)
             per[i]["act"][(0,) * nb + (every, columns)] = (gate / (1.0 + jnp.exp(-gate)) * up_).astype(BF16)
-            issue(act_copy(i, 0, q), c, p.splits[i].send)
+            act_copy(i, 0, q)(c).start()
 
     def gather(i, k, c):
-        for q in range(2):
-            act_copy(i, k - 1, q)(c).wait_recv()
-            if k < nb - 1:
-                issue(act_copy(i, k, q), c, p.splits[i].send)
-        if k == nb - 1:
+        acts_wait(i, k - 1, c, "ra", p.splits[i].recv)
+        if k < nb - 1:
+            make_room(acts_wait, i, k, c, "sa")
+            for q in range(2):
+                act_copy(i, k, q)(c).start()
+        else:
             issue(act_copy(i, k, 0), c, p.splits[i].send)
 
     def down(i, j):
@@ -349,6 +366,8 @@
         act_ = functools.partial(each, t, begin, end)
         if end <= C:
             up(t)
+        if begin == 0:
+            pl.semaphore_wait(barrier, nb + 1 + jnp.where(deep > 0, 1, 0))
         for i, s in enumerate(p.splits):
             act_([(0, J, s.down, 1)], functools.partial(down, i))
             act_(shift(s, 0), lambda c, i=i: issue(sum_copy(i, 0, 0), c, p.splits[i].send))
@@ -373,17 +392,19 @@
         if begin == C:
             for i in range(2):
                 d_copy(0, i).start()
-        lax.fori_loop(begin, end, functools.partial(step, begin, end), 0)
+        if end == begin + 1:
+            step(begin, end, begin, 0)
+        else:
+            lax.fori_loop(begin, end, functools.partial(step, begin, end), 0)
 
     for i in range(len(p.splits)):
         for c in range(max(C - p.splits[i].send, 0), C):
             sum_copy(i, 0, 0)(c).wait_send()
             act_copy(i, nb - 1, 0)(c).wait_send()
-            for q in range(2):
-                for s in range(1, nb):
-                    sum_copy(i, s, q)(c).wait_send()
-                for k in range(nb - 1):
-                    act_copy(i, k, q)(c).wait_send()
+            for s in range(1, nb):
+                sums_wait(i, s, c, "sk", p.splits[i].send)
+            for k in range(nb - 1):
+                acts_wait(i, k, c, "sa", p.splits[i].send)
 
         def finish(j, carry, i=i):
             z_in(i, j).wait_send()
@@ -422,10 +443,10 @@
             "sem": {
                 "s0": dma((s.send,)),
                 "r0": dma((s.recv,)),
-                "sk": dma((nb - 1, 2, s.send)),
-                "rk": dma((nb - 1, 2, s.recv)),
-                "sa": dma((nb - 1, 2, s.send)),
-                "ra": dma((nb - 1, 2, s.recv)),
+                "sk": dma((nb - 1, s.send)),
+                "rk": dma((nb - 1, s.recv)),
+                "sa": dma((nb - 1, s.send)),
+                "ra": dma((nb - 1, s.recv)),
                 "sl": dma((s.send,)),
                 "rl": dma((s.recv,)),
                 "zs": dma((SLOTS,)),

time: 146 us -> 145 us (level)
  Pallas kernels: 143 us -> 141 us
where the time goes in v2:
time: 145 us
  Pallas kernels  141 us (97%)
  local copies, waits for them, and re-layouts  3.16 us (2%)
    pallas_call x1, Pallas kernels, body(): pl.pallas_call(functools.partial(kernel, p), out_shape=jax.ShapeDtypeStru...  141 us
    unnamed x1, local copies, waits for them, and re-layouts  3.16 us

profile of v2, /device:TPU:0, one launch (start us, length us, event | category | flops | bytes accessed | tf_op | source)
XLA Modules:
  0.0 144.6 jit_solution(14360921830989407428)
XLA Ops:
  0.0 141.4 %mlp.1 = bf16[8,64,2048]{2,1,0:T(8,128)(2,1)} custom-call(bf16[8,64,2048]{2,1,0:T(8,128)(2,1)} %bitcast.3, bf16[2048,6656]{1,0:T(8,128)(2,1)} %gc.1, bf16[2048,6656]{1,0:T(8,128)(2,1)} %uc.1, bf16[6656,2048]{1,0:T(8,128)(2,1)} %dc.1, f32[16,6656]{1,0:T(8,128)} %gs.1, f32[16,6656]{1,0:T(8,128)} %us.1, f32[52,2048]{1,0:T(8,128)} %ds.1), custom_call_target="tpu_custom_call" | custom-call | flops 41875931136 | bytes 109051904 | tf_op jit(solution)/shard_map/mlp/pallas_call | solution.py:461
  141.4 3.2 %copy.9 = bf16[512,2048]{1,0:T(8,128)(2,1)} copy(bf16[512,2048]{1,0:T(8,128)(2,1)} %bitcast.2) | data formatting | bytes 4194304

commit v3 on v2

--- a/solution.py
+++ b/solution.py
@@ -105,13 +105,13 @@
         )
 
     def w_copy(c, i):
-        slot = lax.rem(c, 2)
+        slot = lax.rem(c, 3)
         return pltpu.make_async_copy(
             (gc, uc)[i].at[:, columns_of(c)], w.at[slot, pl.ds(i * p.depth, p.depth)], sems["w"].at[slot, i]
         )
 
     def d_copy(v, i):
-        slot = lax.rem(v, 2)
+        slot = lax.rem(v, 3)
         return pltpu.make_async_copy(
             dc.at[pl.ds(i * p.k2, p.k2), columns_at(lax.rem(v, J))],
             w.at[slot, pl.ds(0, p.k2), pl.ds(i * wq, wq)],
@@ -217,7 +217,7 @@
             for i in range(2):
                 w_copy(c + 1, i).start()
 
-        slot = lax.rem(c, 2)
+        slot = lax.rem(c, 3)
         for i, scales in enumerate((gs, us)):
             w_copy(c, i).wait()
             weight = dequant(w[slot, i * p.depth : (i + 1) * p.depth], scales[:, columns_of(c)])
@@ -268,13 +268,13 @@
     def down(i, j):
         v = i * J + j
 
-        @pl.when(v + 1 < J * len(p.splits))
+        @pl.when(v + 2 < J * len(p.splits))
         def _():
             for k in range(2):
-                d_copy(v + 1, k).start()
+                d_copy(v + 2, k).start()
 
         own = per[i]
-        slot = lax.rem(v, 2)
+        slot = lax.rem(v, 3)
         groups = ds.shape[0] // 2
         value = None
         for k in range(2):
@@ -390,8 +390,9 @@
     cuts = sorted(c for c in p.cuts if c < p.ticks) + [p.ticks]
     for begin, end in zip(cuts, cuts[1:]):
         if begin == C:
-            for i in range(2):
-                d_copy(0, i).start()
+            for v in range(2):
+                for i in range(2):
+                    d_copy(v, i).start()
         if end == begin + 1:
             step(begin, end, begin, 0)
         else:
@@ -466,9 +467,9 @@
         scratch_shapes=[
             pltpu.VMEM((n, rows // n, depth), BF16),
             pltpu.VMEM((rows, depth), BF16),
-            pltpu.VMEM((2, p.wrows, p.w), BF16),
+            pltpu.VMEM((3, p.wrows, p.w), BF16),
             [own(s) for s in p.splits],
-            {"x": dma((len(p.splits) * n,)), "w": dma((2, 2))},
+            {"x": dma((len(p.splits) * n,)), "w": dma((3, 2))},
         ],
         compiler_params=pltpu.CompilerParams(collective_id=0, has_side_effects=True, vmem_limit_bytes=67043328),
         cost_estimate=pl.CostEstimate(

time: 145 us -> 144 us (level)
  no operation moved by 1% of the time
where the time goes in v3:
time: 144 us
  Pallas kernels  141 us (98%)
  local copies, waits for them, and re-layouts  3.16 us (2%)
    pallas_call x1, Pallas kernels, body(): pl.pallas_call(functools.partial(kernel, p), out_shape=jax.ShapeDtypeStru...  141 us
    unnamed x1, local copies, waits for them, and re-layouts  3.16 us

profile of v3, /device:TPU:0, one launch (start us, length us, event | category | flops | bytes accessed | tf_op | source)
XLA Modules:
  0.0 143.8 jit_solution(15322789721028188471)
XLA Ops:
  0.0 140.6 %mlp.1 = bf16[8,64,2048]{2,1,0:T(8,128)(2,1)} custom-call(bf16[8,64,2048]{2,1,0:T(8,128)(2,1)} %bitcast.3, bf16[2048,6656]{1,0:T(8,128)(2,1)} %gc.1, bf16[2048,6656]{1,0:T(8,128)(2,1)} %uc.1, bf16[6656,2048]{1,0:T(8,128)(2,1)} %dc.1, f32[16,6656]{1,0:T(8,128)} %gs.1, f32[16,6656]{1,0:T(8,128)} %us.1, f32[52,2048]{1,0:T(8,128)} %ds.1), custom_call_target="tpu_custom_call" | custom-call | flops 41875931136 | bytes 109051904 | tf_op jit(solution)/shard_map/mlp/pallas_call | solution.py:462
  140.6 3.2 %copy.9 = bf16[512,2048]{1,0:T(8,128)(2,1)} copy(bf16[512,2048]{1,0:T(8,128)(2,1)} %bitcast.2) | data formatting | bytes 4194304
